TPU v7x, 128 devices: a whole 4x4x4 slice. The times are simulated.
128 devices in a mesh: row: 8 (over y, core), col: 16 (over x, z).
Axes of the slice: x: 4, y: 4, z: 4, core: 2. Of those that a mesh axis runs over, the one named last changes fastest.
Arguments:
- upper_a: bfloat16 [2, 4096, 8192], P(None, 'row', 'col'), may hold values from -0.125 to 0.125
- upper_b: bfloat16 [4, 4096, 2, 8192], P(None, 'row', None, 'col'), may hold values from -0.125 to 0.125
- right_side: bfloat16 [2, 4096, 2, 8192], P(None, 'row', None, 'col'), may hold values from -6 to 6
- a_bases: bfloat16 [2, 4096, 512], P(None, 'row'), may hold values from -1 to 1, as said below
- b_bases: bfloat16 [2, 8192, 512], P(None, 'col'), may hold values from -1 to 1, as said below
- a_values: float32 [2, 4096], P(None, 'row'), may hold values from 0.25 to 4
- b_values: float32 [2, 8192], P(None, 'col'), may hold values from 0.25 to 4
Outputs:
- solution: float32 [2, 4096, 2, 8192], P(None, 'row', None, 'col')
Inputs may be any that keep to these rules, and one draw needn't show every extreme that they name: Each tile of a_bases is an orthonormal matrix rounded to bfloat16. Each tile of b_bases is an orthonormal matrix rounded to bfloat16.
All inputs are finite; a program needn't handle non-finite values.
Results may differ from a plain program's by a relative error of at most 0.012.
Values may be sent and summed in bfloat16 or wider, within the bound.
A program may use at most 128 MiB of HBM per device.

v0:
```python
import jax
import jax.numpy as jnp
from jax import lax
from jax.sharding import PartitionSpec as P

FRONTS = 4


def passed_along(block, axis, distance):
    devices = range(lax.axis_size(axis))
    route = [((i - distance) % len(devices), i) for i in devices]
    return lax.ppermute(block, axis, route)


def broadcast(value, axis, root):
    return lax.dynamic_index_in_dim(lax.all_gather(value, axis), root, 0, keepdims=False)


def spread(block, axis, holder):
    block = jnp.where(lax.axis_index(axis) == holder, block, jnp.zeros_like(block))
    return lax.psum(block, axis)


def solve_tile(waiting, basis_left, values_left, basis_right, values_right):
    rounded = waiting.astype(jnp.bfloat16)
    first_half = lax.dot_general(
        basis_left, rounded, (((0,), (0,)), ((), ())), preferred_element_type=jnp.float32
    ).astype(jnp.bfloat16)
    scaled = jnp.dot(first_half, basis_right, preferred_element_type=jnp.float32)
    scaled = (scaled / (values_left[:, None] + values_right[None, :])).astype(jnp.bfloat16)
    left_side = jnp.dot(basis_left, scaled, preferred_element_type=jnp.float32).astype(jnp.bfloat16)
    return lax.dot_general(
        left_side, basis_right, (((1,), (1,)), ((), ())), preferred_element_type=jnp.float32
    ).astype(jnp.bfloat16)


def skip_tile(waiting, basis_left, values_left, basis_right, values_right):
    return jnp.zeros(waiting.shape, jnp.bfloat16)


def shift_columns(block, offset):
    return passed_along(block, "col", offset)


def shift_used(block, offset):
    return passed_along(block, "row", offset)


def shards(upper_a, upper_b, right_side, a_bases, b_bases, a_values, b_values):
    row_count = lax.axis_size("row")
    col_count = lax.axis_size("col")
    row_id = lax.axis_index("row")
    col_id = lax.axis_index("col")
    tile_rows = right_side.shape[0]
    tile_cols = right_side.shape[2]
    b_local_rows = upper_b.shape[0]
    first_front = col_count - 2
    rows_glob = jnp.arange(tile_rows, dtype=jnp.int32) * row_count + row_id
    cols_glob = jnp.arange(tile_cols, dtype=jnp.int32) * col_count + col_id
    working = right_side.astype(jnp.float32)
    a_blocks = []
    for front_step in range(FRONTS):
        if front_step == 1:
            a_blocks.append(upper_a)
        else:
            a_blocks.append(shift_columns(upper_a, front_step - 1))
    b_blocks = []
    for front_step in range(FRONTS):
        target_row = (row_id + 1 - front_step) % row_count
        target_glob = jnp.arange(tile_rows, dtype=jnp.int32) * row_count + target_row
        picks = jnp.clip((front_step - 1 + target_glob) // row_count, 0, b_local_rows - 1)
        chosen = jnp.take(upper_b, picks, axis=0)
        if front_step == 1:
            b_blocks.append(chosen)
        else:
            b_blocks.append(shift_used(chosen, 1 - front_step))
    front_of = (col_count - 1 - rows_glob)[:, None] + cols_glob[None, :]
    for front_step in range(FRONTS):
        front_id = first_front + front_step
        owned = front_of == front_id
        holder = jnp.any(owned)
        flat_index = jnp.argmax(owned.reshape(-1).astype(jnp.int32))
        a_pick = flat_index // tile_cols
        b_pick = flat_index % tile_cols
        waiting = working[a_pick, :, b_pick, :]
        x_tile = lax.cond(
            holder,
            solve_tile,
            skip_tile,
            waiting,
            a_bases[a_pick],
            a_values[a_pick],
            b_bases[b_pick],
            b_values[b_pick],
        )
        working = working.at[a_pick, :, b_pick, :].set(
            jnp.where(holder, x_tile.astype(jnp.float32), waiting)
        )
        column_x = broadcast(x_tile, "row", (1 - front_step + col_id) % row_count)
        row_list = []
        for row_part in range(tile_rows):
            root_col = (front_step - 1 + row_part * row_count + row_id) % col_count
            row_list.append(spread(x_tile, "col", root_col))
        row_x = jnp.stack(row_list)
        k_glob = col_count - 1 - front_id + cols_glob
        k_valid = (k_glob >= 0) & (k_glob <= col_count - 1)
        column_mask = (k_valid[None, :] & (rows_glob[:, None] < k_glob[None, :])).astype(
            jnp.float32
        )
        column_terms = jnp.einsum(
            "apq,qr->apr", a_blocks[front_step], column_x, preferred_element_type=jnp.float32
        )
        l_glob = front_id - col_count + 1 + rows_glob
        row_mask = ((l_glob[:, None] >= 0) & (l_glob[:, None] < cols_glob[None, :])).astype(
            jnp.float32
        )
        row_terms = jnp.einsum(
            "apq,aqbr->apbr", row_x, b_blocks[front_step], preferred_element_type=jnp.float32
        )
        working = (
            working
            - column_terms[:, :, None, :] * column_mask[:, None, :, None]
            - row_terms * row_mask[:, None, :, None]
        )
    return working


def solution(mesh):
    return jax.shard_map(
        shards,
        mesh=mesh,
        in_specs=(
            P(None, "row", "col"),
            P(None, "row", None, "col"),
            P(None, "row", None, "col"),
            P(None, "row", None),
            P(None, "col", None),
            P(None, "row"),
            P(None, "col"),
        ),
        out_specs=P(None, "row", None, "col"),
        check_vma=False,
    )
```

profile of v0, /device:TPU:0, one launch (start us, length us, event | category | flops | bytes accessed | tf_op | source)
XLA Modules:
  0.0 492.8 jit_solution(4523634216439111667)
XLA Ops:
  7.5 0.8 and_convert_fusion.1
  11.5 4.3 copy_convert_fusion
  16.5 2.3 dynamic-slice_bitcast_fusion.3
  18.9 0.8 copy-done.2
  19.8 7.0 %gather_fusion = bf16[2,512,2,512]{3,2,1,0:T(2,128)(2,1)S(1)} fusion(bf16[4,512,2,512]{3,2,1,0:T(2,128)(2,1)} %param.26, s32[1024]{0:T(1024)S(1)} %pad_clamp_fusion.3), kind=kCustom, calls=%fused_computation.clone | custom fusion | bytes 4194312 | tf_op jit(solution)/shard_map/jit(_take)/gather | solution.py:72
  26.9 1.7 copy_select_fusion.2
  28.6 3.0 collective-permute-start.1
  31.5 3.4 collective-permute-start
  34.9 1.1 select_bitcast_fusion.7
  36.1 0.7 iota_reduce_fusion.2
  39.9 0.7 and_reduce_fusion.2
  40.7 3.9 fusion.88
  44.6 17.6 %collective-permute-done = bf16[2,512,512]{2,1,0:T(8,128)(2,1)S(1)} collective-permute-done((bf16[2,512,512]{2,1,0:T(8,128)(2,1)}, bf16[2,512,512]{2,1,0:T(8,128)(2,1)S(1)}, u32[]{:S(2)}, u32[]{:S(2)}) %collective-permute-start) | collective-permute-done | bytes 1048608 | tf_op jit(solution)/shard_map/ppermute | solution.py:12
  62.3 4.6 all-gather.9.cloned.1.call-done
  66.8 3.2 convolution_bitcast_fusion.3
  70.0 1.9 copy.21
  71.9 59.6 %all-reduce.15.cloned.1.call-done = (bf16[1,512,512]{2,1,0:T(8,128)(2,1)}, bf16[1,512,512]{2,1,0:T(8,128)(2,1)}) async-done(((bf16[1,512,512]{2,1,0:T(8,128)(2,1)}, bf16[1,512,512]{2,1,0:T(8,128)(2,1)}), (bf16[1,512,512]{2,1,0:T(8,128)(2,1)}, bf16[1,512,512]{2,1,0:T(8,128)(2,1)})) %all-reduce.15.cloned.1.call-update) | async-done | bytes 1048592 | tf_op jit(solution)/shard_map/psum | solution.py:21
  131.5 6.5 %multiply_subtract_fusion.3 = f32[2,512,2,512]{3,1,2,0:T(8,128)} fusion(f32[2,512,2,512]{3,1,2,0:T(8,128)} %fusion.88, bf16[2,512,2,512]{3,1,2,0:T(8,128)(2,1)} %collective-permute-done.1, f32[2,2]{1,0:T(2,128)S(1)} %get-tuple-element.403, f32[2,2]{1,0:T(2,128)S(1)} %get-tuple-element.390, f32[2,512,512]{2,1,0:T(8,128)S(1)} %copy.21, ...), kind=kOutput, calls=%fused_computation.79 | convolution fusion | flops 1080033280 | bytes 13631520 | tf_op jit(solution)/shard_map/apq,aqbr->apbr/dot_general | solution.py:117
  138.0 2.4 dynamic-slice_bitcast_fusion.2
  140.5 2.7 conditional.5
  140.5 2.0 fusion.19
  142.5 0.7 convolution_convert_fusion.3
  143.2 0.8 copy-done.4
  147.6 8.0 %gather_fusion.1 = bf16[2,512,2,512]{3,2,1,0:T(2,128)(2,1)} fusion(bf16[4,512,2,512]{3,2,1,0:T(2,128)(2,1)} %param.26, s32[1024]{0:T(1024)S(1)} %pad_clamp_fusion.2), kind=kCustom, calls=%fused_computation.1.clone | custom fusion | bytes 4194312 | tf_op jit(solution)/shard_map/jit(_take)/gather | solution.py:72
  156.1 1.1 select_bitcast_fusion.5
  157.2 3.5 broadcast_select_fusion
  160.7 3.7 fusion.87
  164.4 10.4 %all-gather.11.cloned.1.call-done = bf16[4096,512]{1,0:T(8,128)(2,1)} async-done(((bf16[512,512]{1,0:T(8,128)(2,1)}), bf16[4096,512]{1,0:T(8,128)(2,1)}) %all-gather.11.cloned.1.call-update) | async-done | bytes 4194320 | tf_op jit(solution)/shard_map/all_gather | solution.py:16
  174.9 3.5 convolution_bitcast_fusion.2
  178.4 2.9 copy.24
  181.3 61.7 %all-reduce.13.cloned.1.call-done = (bf16[1,512,512]{2,1,0:T(8,128)(2,1)}, bf16[1,512,512]{2,1,0:T(8,128)(2,1)}) async-done(((bf16[1,512,512]{2,1,0:T(8,128)(2,1)}, bf16[1,512,512]{2,1,0:T(8,128)(2,1)}), (bf16[1,512,512]{2,1,0:T(8,128)(2,1)}, bf16[1,512,512]{2,1,0:T(8,128)(2,1)})) %all-reduce.13.cloned.1.call-update) | async-done | bytes 1048592 | tf_op jit(solution)/shard_map/psum | solution.py:21
  243.0 4.6 multiply_subtract_fusion.2
  247.6 2.0 copy-done
  249.6 1.1 dynamic-slice_bitcast_fusion.1
  251.3 0.8 copy-done.6
  252.2 7.0 %gather_fusion.2 = bf16[2,512,2,512]{3,2,1,0:T(2,128)(2,1)S(1)} fusion(bf16[4,512,2,512]{3,2,1,0:T(2,128)(2,1)} %param.26, s32[1024]{0:T(1024)S(1)} %pad_clamp_fusion.1), kind=kCustom, calls=%fused_computation.2.clone | custom fusion | bytes 4194312 | tf_op jit(solution)/shard_map/jit(_take)/gather | solution.py:72
  259.3 1.7 copy_select_fusion.1
  261.0 3.9 collective-permute-start.3
  265.0 0.9 collective-permute-start.2
  265.9 1.1 select_bitcast_fusion.3
  271.1 0.7 and_reduce_fusion
  271.9 4.1 fusion.86
  276.0 18.3 %collective-permute-done.2 = bf16[2,512,512]{2,1,0:T(8,128)(2,1)S(1)} collective-permute-done((bf16[2,512,512]{2,1,0:T(8,128)(2,1)}, bf16[2,512,512]{2,1,0:T(8,128)(2,1)S(1)}, u32[]{:S(2)}, u32[]{:S(2)}) %collective-permute-start.2) | collective-permute-done | bytes 1048608 | tf_op jit(solution)/shard_map/ppermute | solution.py:12
  294.4 3.2 convolution_bitcast_fusion.1
  297.5 1.9 copy.27
  299.4 4.8 collective-permute-done.3
  304.2 55.2 %all-reduce.11.cloned.1.call-done = (bf16[1,512,512]{2,1,0:T(8,128)(2,1)}, bf16[1,512,512]{2,1,0:T(8,128)(2,1)}) async-done(((bf16[1,512,512]{2,1,0:T(8,128)(2,1)}, bf16[1,512,512]{2,1,0:T(8,128)(2,1)}), (bf16[1,512,512]{2,1,0:T(8,128)(2,1)}, bf16[1,512,512]{2,1,0:T(8,128)(2,1)})) %all-reduce.11.cloned.1.call-update) | async-done | bytes 1048592 | tf_op jit(solution)/shard_map/psum | solution.py:21
  359.4 4.5 multiply_subtract_fusion.1
  364.0 2.0 copy-done.1
  366.0 1.1 dynamic-slice_bitcast_fusion
  367.9 0.8 copy-done.8
  368.8 7.0 %gather_fusion.3 = bf16[2,512,2,512]{3,2,1,0:T(2,128)(2,1)S(1)} fusion(bf16[4,512,2,512]{3,2,1,0:T(2,128)(2,1)} %param.26, s32[1024]{0:T(1024)S(1)} %pad_clamp_fusion), kind=kCustom, calls=%fused_computation.3.clone | custom fusion | bytes 4194312 | tf_op jit(solution)/shard_map/jit(_take)/gather | solution.py:72
  375.9 1.7 copy_select_fusion
  377.6 5.5 %collective-permute-start.5 = (bf16[2,512,2,512]{3,1,2,0:T(8,128)(2,1)}, bf16[2,512,2,512]{3,1,2,0:T(8,128)(2,1)}, u32[]{:S(2)}, u32[]{:S(2)}) collective-permute-start(bf16[2,512,2,512]{3,1,2,0:T(8,128)(2,1)} %copy_select_fusion), channel_id=1, source_target_pairs={{32,0},{48,16},{64,32},{80,48},{96,64},{112,80},{0,96},{16,112},{3... | collective-permute-start | bytes 6291464 | tf_op jit(solution)/shard_map/ppermute | solution.py:12
  383.1 1.1 select_bitcast_fusion.1
  384.2 4.0 fusion.85
  388.2 22.6 %collective-permute-done.4 = bf16[2,512,512]{2,1,0:T(8,128)(2,1)S(1)} collective-permute-done((bf16[2,512,512]{2,1,0:T(8,128)(2,1)}, bf16[2,512,512]{2,1,0:T(8,128)(2,1)S(1)}, u32[]{:S(2)}, u32[]{:S(2)}) %collective-permute-start.4) | collective-permute-done | bytes 1048608 | tf_op jit(solution)/shard_map/ppermute | solution.py:12
  410.9 7.6 %all-gather.15.cloned.1.call-done = bf16[4096,512]{1,0:T(8,128)(2,1)} async-done(((bf16[512,512]{1,0:T(8,128)(2,1)}), bf16[4096,512]{1,0:T(8,128)(2,1)}) %all-gather.15.cloned.1.call-update) | async-done | bytes 4194320 | tf_op jit(solution)/shard_map/all_gather | solution.py:16
  418.5 3.2 convolution_bitcast_fusion
  421.6 1.9 copy.30
  423.6 16.7 %collective-permute-done.5 = bf16[2,512,2,512]{3,1,2,0:T(8,128)(2,1)} collective-permute-done((bf16[2,512,2,512]{3,1,2,0:T(8,128)(2,1)}, bf16[2,512,2,512]{3,1,2,0:T(8,128)(2,1)}, u32[]{:S(2)}, u32[]{:S(2)}) %collective-permute-start.5) | collective-permute-done | bytes 2097184 | tf_op jit(solution)/shard_map/ppermute | solution.py:12
  440.3 35.4 %all-reduce.9.cloned.1.call-done = (bf16[1,512,512]{2,1,0:T(8,128)(2,1)}, bf16[1,512,512]{2,1,0:T(8,128)(2,1)}) async-done(((bf16[1,512,512]{2,1,0:T(8,128)(2,1)}, bf16[1,512,512]{2,1,0:T(8,128)(2,1)}), (bf16[1,512,512]{2,1,0:T(8,128)(2,1)}, bf16[1,512,512]{2,1,0:T(8,128)(2,1)})) %all-reduce.9.cloned.1.call-update) | async-done | bytes 1048592 | tf_op jit(solution)/shard_map/psum | solution.py:21
  475.6 4.5 multiply_subtract_fusion
  480.2 5.2 %copy.32 = f32[2,512,2,512]{3,2,1,0:T(2,128)} copy(f32[2,512,2,512]{3,1,2,0:T(8,128)S(1)} %multiply_subtract_fusion) | data formatting | bytes 8388608 | tf_op jit(solution)/shard_map/sub | solution.py:121
  (83 shorter events, 5.0 us)
Async XLA Ops:
  7.4 59.5 %all-gather.9.cloned.1.call-start = ((), (), s32[]{:S(2)}) async-start(), calls=%async_computation | async-start | bytes 4718592 | tf_op jit(solution)/shard_map/all_gather | solution.py:16
  15.8 3.0 copy-start.10
  15.8 3.0 copy-start.11
  15.8 3.0 copy-start.13
  18.9 0.8 copy-start.2
  19.7 111.8 %all-reduce.15.cloned.1.call-start = ((), (), s32[]{:S(2)}) async-start(), calls=%async_computation.7 | async-start | bytes 2097152 | tf_op jit(solution)/shard_map/psum | solution.py:21
  26.8 8.1 %copy-start.3 = (bf16[512,512]{1,0:T(8,128)(2,1)S(1)}, bf16[512,512]{1,0:T(8,128)(2,1)}, u32[]{:S(2)}) copy-start(bf16[512,512]{1,0:T(8,128)(2,1)} %copy-done.2) | copy-start | bytes 1572868
  28.6 11.4 %copy-start.12 = (s32[4]{0:T(128)S(1)}, s32[4]{0:T(128)}, u32[]{:S(2)}) copy-start(s32[4]{0:T(128)} %constant.378.clone.1) | copy-start | bytes 52
  28.6 103.0 %collective-permute-start.1 = (bf16[2,512,2,512]{3,1,2,0:T(8,128)(2,1)}, bf16[2,512,2,512]{3,1,2,0:T(8,128)(2,1)}, u32[]{:S(2)}, u32[]{:S(2)}) collective-permute-start(bf16[2,512,2,512]{3,1,2,0:T(8,128)(2,1)} %copy_select_fusion.2), channel_id=1, source_target_pairs={{112,0},{0,16},{16,32},{32,48},{48,64},{64,80},{80,96},{96,112},{1... | collective-permute-start | bytes 6291464 | tf_op jit(solution)/shard_map/ppermute | solution.py:12
  31.5 30.7 %collective-permute-start = (bf16[2,512,512]{2,1,0:T(8,128)(2,1)}, bf16[2,512,512]{2,1,0:T(8,128)(2,1)S(1)}, u32[]{:S(2)}, u32[]{:S(2)}) collective-permute-start(bf16[2,512,512]{2,1,0:T(8,128)(2,1)} %param.25), channel_id=1, source_target_pairs={{1,0},{2,1},{3,2},{4,3},{5,4},{6,5},{7,6},{8,7},{9,8},{10,9},{11,1... | collective-permute-start | bytes 3145736 | tf_op jit(solution)/shard_map/ppermute | solution.py:12
  36.0 138.9 %all-gather.11.cloned.1.call-start = ((), (), s32[]{:S(2)}) async-start(), calls=%async_computation.1 | async-start | bytes 4718592 | tf_op jit(solution)/shard_map/all_gather | solution.py:16
  138.0 2.4 copy-start.14
  138.0 2.4 copy-start.17
  143.2 0.8 copy-start.4
  144.0 99.0 %all-reduce.13.cloned.1.call-start = ((), (), s32[]{:S(2)}) async-start(), calls=%async_computation.6 | async-start | bytes 2097152 | tf_op jit(solution)/shard_map/psum | solution.py:21
  147.5 8.6 %copy-start.5 = (bf16[512,512]{1,0:T(8,128)(2,1)S(1)}, bf16[512,512]{1,0:T(8,128)(2,1)}, u32[]{:S(2)}) copy-start(bf16[512,512]{1,0:T(8,128)(2,1)} %copy-done.4) | copy-start | bytes 1572868
  157.2 137.2 %all-gather.13.cloned.1.call-start = ((), (), s32[]{:S(2)}) async-start(), calls=%async_computation.2 | async-start | bytes 4718592 | tf_op jit(solution)/shard_map/all_gather | solution.py:16
  247.6 2.0 copy-start
  249.6 1.6 copy-start.15
  251.3 0.8 copy-start.6
  252.1 107.3 %all-reduce.11.cloned.1.call-start = ((), (), s32[]{:S(2)}) async-start(), calls=%async_computation.5 | async-start | bytes 2097152 | tf_op jit(solution)/shard_map/psum | solution.py:21
  259.3 6.6 %copy-start.7 = (bf16[512,512]{1,0:T(8,128)(2,1)S(1)}, bf16[512,512]{1,0:T(8,128)(2,1)}, u32[]{:S(2)}) copy-start(bf16[512,512]{1,0:T(8,128)(2,1)} %copy-done.6) | copy-start | bytes 1572868
  261.0 43.2 %collective-permute-start.3 = (bf16[2,512,2,512]{3,1,2,0:T(8,128)(2,1)}, bf16[2,512,2,512]{3,1,2,0:T(8,128)(2,1)}, u32[]{:S(2)}, u32[]{:S(2)}) collective-permute-start(bf16[2,512,2,512]{3,1,2,0:T(8,128)(2,1)} %copy_select_fusion.1), channel_id=1, source_target_pairs={{16,0},{32,16},{48,32},{64,48},{80,64},{96,80},{112,96},{0,112},{1... | collective-permute-start | bytes 6291464 | tf_op jit(solution)/shard_map/ppermute | solution.py:12
  265.0 29.4 %collective-permute-start.2 = (bf16[2,512,512]{2,1,0:T(8,128)(2,1)}, bf16[2,512,512]{2,1,0:T(8,128)(2,1)S(1)}, u32[]{:S(2)}, u32[]{:S(2)}) collective-permute-start(bf16[2,512,512]{2,1,0:T(8,128)(2,1)} %param.25), channel_id=1, source_target_pairs={{15,0},{0,1},{1,2},{2,3},{3,4},{4,5},{5,6},{6,7},{7,8},{8,9},{9,10... | collective-permute-start | bytes 3145736 | tf_op jit(solution)/shard_map/ppermute | solution.py:12
  267.0 151.5 %all-gather.15.cloned.1.call-start = ((), (), s32[]{:S(2)}) async-start(), calls=%async_computation.3 | async-start | bytes 4718592 | tf_op jit(solution)/shard_map/all_gather | solution.py:16
  363.9 2.0 copy-start.1
  366.0 1.6 copy-start.16
  366.0 1.9 copy-start.18
  367.9 0.8 copy-start.8
  368.7 106.9 %all-reduce.9.cloned.1.call-start = ((), (), s32[]{:S(2)}) async-start(), calls=%async_computation.4 | async-start | bytes 2097152 | tf_op jit(solution)/shard_map/psum | solution.py:21
  375.9 7.2 %copy-start.9 = (bf16[512,512]{1,0:T(8,128)(2,1)S(1)}, bf16[512,512]{1,0:T(8,128)(2,1)}, u32[]{:S(2)}) copy-start(bf16[512,512]{1,0:T(8,128)(2,1)} %copy-done.8) | copy-start | bytes 1572868
  377.6 62.7 %collective-permute-start.5 = (bf16[2,512,2,512]{3,1,2,0:T(8,128)(2,1)}, bf16[2,512,2,512]{3,1,2,0:T(8,128)(2,1)}, u32[]{:S(2)}, u32[]{:S(2)}) collective-permute-start(bf16[2,512,2,512]{3,1,2,0:T(8,128)(2,1)} %copy_select_fusion), channel_id=1, source_target_pairs={{32,0},{48,16},{64,32},{80,48},{96,64},{112,80},{0,96},{16,112},{3... | collective-permute-start | bytes 6291464 | tf_op jit(solution)/shard_map/ppermute | solution.py:12
  383.1 27.8 %collective-permute-start.4 = (bf16[2,512,512]{2,1,0:T(8,128)(2,1)}, bf16[2,512,512]{2,1,0:T(8,128)(2,1)S(1)}, u32[]{:S(2)}, u32[]{:S(2)}) collective-permute-start(bf16[2,512,512]{2,1,0:T(8,128)(2,1)} %param.25), channel_id=1, source_target_pairs={{14,0},{15,1},{0,2},{1,3},{2,4},{3,5},{4,6},{5,7},{6,8},{7,9},{8,1... | collective-permute-start | bytes 3145736 | tf_op jit(solution)/shard_map/ppermute | solution.py:12
Sparse Core Ops, SparseCore 0:
  19.8 46.9 all-gather.8
  144.1 30.7 all-gather.10
  252.2 41.5 all-gather.12
  368.9 49.5 all-gather.14
Sparse Core Ops, SparseCore 1:
  36.1 95.4 all-reduce.14
  157.3 85.7 all-reduce.12
  267.1 92.3 all-reduce.10
  384.3 91.3 all-reduce.8
where the time goes:
time: 494 us; the launch traced here: 493 us
  waiting for transfers between devices  315 us (64%)
  local copies, waits for them, and re-layouts  58.9 us (12%)
  other arithmetic  38.2 us (8%)
  matrix products  35.8 us (7%)
  between operations  27.7 us (6%)
  starting transfers between devices  17.4 us (4%)
    psum x4, waiting for transfers between devices, spread(): return lax.psum(block, axis)  212 us
    ppermute x6, waiting for transfers between devices, passed_along(): return lax.ppermute(block, axis, route)  80.1 us
    gather x4, local copies, waits for them, and re-layouts, shards(): chosen = jnp.take(upper_b, picks, axis=0)  29.1 us
    all_gather x4, waiting for transfers between devices, broadcast(): lax.all_gather(value, axis)  22.6 us
    dot_general x4, matrix products, shards(): jnp.einsum('apq,aqbr->apbr', row_x, b_blocks[front_step], preferred_eleme...  20.2 us
    ppermute x6, starting transfers between devices, passed_along(): return lax.ppermute(block, axis, route)  16.7 us
    scatter x4, other arithmetic, shards(): working.at[a_pick, :, b_pick, :]  15.9 us
    dot_general x4, matrix products, shards(): jnp.einsum('apq,qr->apr', a_blocks[front_step], column_x, preferred_eleme...  12.9 us
  transfers between devices with their start and end apart: 14, of which 12 were waited for; matrix products, arithmetic and copies ran while one was open for 17% of the time, Pallas kernels for 0%

commit v1 on v0

--- a/solution.py
+++ b/solution.py
@@ -4,6 +4,7 @@
 from jax.sharding import PartitionSpec as P
 
 FRONTS = 4
+match_sums_all_over_axis = lambda z, named_axis: jnp.sum(lax.all_gather(z, named_axis), 0)
 
 
 def passed_along(block, axis, distance):
@@ -18,7 +19,7 @@
 
 def spread(block, axis, holder):
     block = jnp.where(lax.axis_index(axis) == holder, block, jnp.zeros_like(block))
-    return lax.psum(block, axis)
+    return match_sums_all_over_axis(block, axis)
 
 
 def solve_tile(waiting, basis_left, values_left, basis_right, values_right):

time: 494 us -> 850 us (1.72); the launches traced: 493 us -> 840 us
  waiting for transfers between devices: 315 us -> 619 us
  other arithmetic: 38.2 us -> 81.3 us
    all_gather x0 -> x8, waiting for transfers between devices: none -> 543 us  [lax.all_gather(z, named_axis)]
    psum x4 -> x0, waiting for transfers between devices: 212 us -> none  [spread(): return lax.psum(block, axis)]
    reduce_sum x0 -> x8, other arithmetic: none -> 38.6 us  [jnp.sum(lax.all_gather(z, named_axis), 0)]
    ppermute x6, waiting for transfers between devices: 80.1 us -> 49.3 us  [passed_along(): return lax.ppermute(block, axis, route)]
  transfers between devices with their start and end apart: 14 -> 18, of which waited for: 12 -> 15; matrix products, arithmetic and copies ran while one was open for 17% -> 14% of each run, Pallas kernels for 0% -> 0%
where the time goes in v1:
time: 850 us; the launch traced here: 840 us
  waiting for transfers between devices  619 us (73%)
  other arithmetic  81.3 us (10%)
  local copies, waits for them, and re-layouts  57.9 us (7%)
  matrix products  35 us (4%)
  between operations  26.8 us (3%)
  starting transfers between devices  19.1 us (2%)
    all_gather x8, waiting for transfers between devices, lax.all_gather(z, named_axis)  543 us
    ppermute x6, waiting for transfers between devices, passed_along(): return lax.ppermute(block, axis, route)  49.3 us
    reduce_sum x8, other arithmetic, jnp.sum(lax.all_gather(z, named_axis), 0)  38.6 us
    gather x4, local copies, waits for them, and re-layouts, shards(): chosen = jnp.take(upper_b, picks, axis=0)  29.3 us
    all_gather x4, waiting for transfers between devices, broadcast(): lax.all_gather(value, axis)  25.1 us
    dot_general x4, matrix products, shards(): jnp.einsum('apq,aqbr->apbr', row_x, b_blocks[front_step], preferred_eleme...  18.9 us
    ppermute x6, starting transfers between devices, passed_along(): return lax.ppermute(block, axis, route)  18.5 us
  transfers between devices with their start and end apart: 18, of which 15 were waited for; matrix products, arithmetic and copies ran while one was open for 14% of the time, Pallas kernels for 0%

profile of v1, /device:TPU:0, one launch (start us, length us, event | category | flops | bytes accessed | tf_op | source)
XLA Modules:
  0.0 840.1 jit_solution(12779200254105849636)
XLA Ops:
  10.6 4.4 copy_convert_fusion
  15.6 2.4 dynamic-slice_bitcast_fusion.3
  19.0 2.1 broadcast_select_fusion.8
  22.0 7.1 gather_fusion
  29.1 1.7 copy_select_fusion.2
  30.8 3.6 collective-permute-start.1
  34.4 2.7 collective-permute-start
  42.1 4.0 fusion.88
  46.0 14.2 %collective-permute-done = bf16[2,512,512]{2,1,0:T(8,128)(2,1)S(1)} collective-permute-done((bf16[2,512,512]{2,1,0:T(8,128)(2,1)}, bf16[2,512,512]{2,1,0:T(8,128)(2,1)S(1)}, u32[]{:S(2)}, u32[]{:S(2)}) %collective-permute-start) | collective-permute-done | bytes 1048608 | tf_op jit(solution)/shard_map/ppermute | solution.py:13
  60.3 6.4 all-gather.25.cloned.1.call-done
  66.6 3.2 convolution_bitcast_fusion.3
  69.8 1.9 copy.21
  71.8 67.1 %all-gather.27.cloned.1.call-done = bf16[8192,512]{1,0:T(8,128)(2,1)} async-done(((bf16[512,512]{1,0:T(8,128)(2,1)}), bf16[8192,512]{1,0:T(8,128)(2,1)}) %all-gather.27.cloned.1.call-update) | async-done | bytes 8388624 | tf_op jit(solution)/shard_map/all_gather | solution.py:7
  138.8 4.8 reduce_sum.96
  143.7 67.9 %all-gather.29.cloned.1.call-done = bf16[8192,512]{1,0:T(8,128)(2,1)} async-done(((bf16[512,512]{1,0:T(8,128)(2,1)}), bf16[8192,512]{1,0:T(8,128)(2,1)}) %all-gather.29.cloned.1.call-update) | async-done | bytes 8388624 | tf_op jit(solution)/shard_map/all_gather | solution.py:7
  211.5 4.8 reduce_sum.97
  216.4 6.2 multiply_subtract_fusion.3
  222.6 2.3 dynamic-slice_bitcast_fusion.2
  224.9 3.6 conditional.5
  225.3 2.4 fusion.19
  229.4 2.1 broadcast_select_fusion.6
  235.2 8.0 gather_fusion.1
  243.9 3.5 broadcast_select_fusion
  247.5 3.8 fusion.87
  251.2 9.4 %all-gather.31.cloned.1.call-done = bf16[4096,512]{1,0:T(8,128)(2,1)} async-done(((bf16[512,512]{1,0:T(8,128)(2,1)}), bf16[4096,512]{1,0:T(8,128)(2,1)}) %all-gather.31.cloned.1.call-update) | async-done | bytes 4194320 | tf_op jit(solution)/shard_map/all_gather | solution.py:17
  260.6 3.5 convolution_bitcast_fusion.2
  264.1 2.9 copy.24
  267.0 66.5 %all-gather.33.cloned.1.call-done = bf16[8192,512]{1,0:T(8,128)(2,1)} async-done(((bf16[512,512]{1,0:T(8,128)(2,1)}), bf16[8192,512]{1,0:T(8,128)(2,1)}) %all-gather.33.cloned.1.call-update) | async-done | bytes 8388624 | tf_op jit(solution)/shard_map/all_gather | solution.py:7
  333.5 4.8 reduce_sum.98
  338.3 67.7 %all-gather.35.cloned.1.call-done = bf16[8192,512]{1,0:T(8,128)(2,1)} async-done(((bf16[512,512]{1,0:T(8,128)(2,1)}), bf16[8192,512]{1,0:T(8,128)(2,1)}) %all-gather.35.cloned.1.call-update) | async-done | bytes 8388624 | tf_op jit(solution)/shard_map/all_gather | solution.py:7
  406.0 4.8 reduce_sum.99
  410.9 4.3 multiply_subtract_fusion.2
  415.2 2.0 copy-done
  417.2 1.1 dynamic-slice_bitcast_fusion.1
  419.5 2.1 broadcast_select_fusion.4
  422.5 7.1 gather_fusion.2
  429.6 1.7 copy_select_fusion.1
  431.3 6.1 collective-permute-start.3
  442.2 4.2 fusion.86
  446.3 14.0 %collective-permute-done.2 = bf16[2,512,512]{2,1,0:T(8,128)(2,1)S(1)} collective-permute-done((bf16[2,512,512]{2,1,0:T(8,128)(2,1)}, bf16[2,512,512]{2,1,0:T(8,128)(2,1)S(1)}, u32[]{:S(2)}, u32[]{:S(2)}) %collective-permute-start.2) | collective-permute-done | bytes 1048608 | tf_op jit(solution)/shard_map/ppermute | solution.py:13
  460.4 1.4 all-gather.37.cloned.1.call-done
  461.8 3.2 convolution_bitcast_fusion.1
  465.0 1.9 copy.27
  466.9 69.0 %all-gather.39.cloned.1.call-done = bf16[8192,512]{1,0:T(8,128)(2,1)} async-done(((bf16[512,512]{1,0:T(8,128)(2,1)}), bf16[8192,512]{1,0:T(8,128)(2,1)}) %all-gather.39.cloned.1.call-update) | async-done | bytes 8388624 | tf_op jit(solution)/shard_map/all_gather | solution.py:7
  535.9 4.8 reduce_sum.100
  540.7 67.9 %all-gather.41.cloned.1.call-done = bf16[8192,512]{1,0:T(8,128)(2,1)} async-done(((bf16[512,512]{1,0:T(8,128)(2,1)}), bf16[8192,512]{1,0:T(8,128)(2,1)}) %all-gather.41.cloned.1.call-update) | async-done | bytes 8388624 | tf_op jit(solution)/shard_map/all_gather | solution.py:7
  608.6 4.8 reduce_sum.101
  613.4 4.2 multiply_subtract_fusion.1
  617.6 2.0 copy-done.1
  621.7 2.1 broadcast_select_fusion.2
  624.4 7.1 gather_fusion.3
  631.5 1.7 copy_select_fusion
  633.2 5.9 collective-permute-start.5
  639.2 4.0 fusion.85
  643.3 21.0 %collective-permute-done.4 = bf16[2,512,512]{2,1,0:T(8,128)(2,1)S(1)} collective-permute-done((bf16[2,512,512]{2,1,0:T(8,128)(2,1)}, bf16[2,512,512]{2,1,0:T(8,128)(2,1)S(1)}, u32[]{:S(2)}, u32[]{:S(2)}) %collective-permute-start.4) | collective-permute-done | bytes 1048608 | tf_op jit(solution)/shard_map/ppermute | solution.py:13
  664.3 7.9 all-gather.43.cloned.1.call-done
  672.2 3.2 convolution_bitcast_fusion
  675.4 1.9 copy.30
  677.3 69.0 %all-gather.45.cloned.1.call-done = bf16[8192,512]{1,0:T(8,128)(2,1)} async-done(((bf16[512,512]{1,0:T(8,128)(2,1)}), bf16[8192,512]{1,0:T(8,128)(2,1)}) %all-gather.45.cloned.1.call-update) | async-done | bytes 8388624 | tf_op jit(solution)/shard_map/all_gather | solution.py:7
  746.2 4.8 reduce_sum.102
  751.1 67.7 %all-gather.47.cloned.1.call-done = bf16[8192,512]{1,0:T(8,128)(2,1)} async-done(((bf16[512,512]{1,0:T(8,128)(2,1)}), bf16[8192,512]{1,0:T(8,128)(2,1)}) %all-gather.47.cloned.1.call-update) | async-done | bytes 8388624 | tf_op jit(solution)/shard_map/all_gather | solution.py:7
  818.8 4.8 reduce_sum.103
  823.6 4.2 multiply_subtract_fusion
  827.8 5.2 copy.32
  (99 shorter events, 14.4 us)
Async XLA Ops:
  6.5 60.1 %all-gather.25.cloned.1.call-start = ((), (), s32[]{:S(2)}) async-start(), calls=%async_computation | async-start | bytes 4718592 | tf_op jit(solution)/shard_map/all_gather | solution.py:17
  10.6 7.4 copy-start.10
  10.6 7.4 copy-start.11
  10.6 7.4 copy-start.13
  10.6 7.4 copy-start.17
  18.1 0.8 copy-start.2
  18.9 120.0 %all-gather.27.cloned.1.call-start = ((), (), s32[]{:S(2)}) async-start(), calls=%async_computation.1 | async-start | bytes 8912896 | tf_op jit(solution)/shard_map/all_gather | solution.py:7
  21.1 190.4 %all-gather.29.cloned.1.call-start = ((), (), s32[]{:S(2)}) async-start(), calls=%async_computation.2 | async-start | bytes 8912896 | tf_op jit(solution)/shard_map/all_gather | solution.py:7
  21.9 238.7 %all-gather.31.cloned.1.call-start = ((), (), s32[]{:S(2)}) async-start(), calls=%async_computation.3 | async-start | bytes 4718592 | tf_op jit(solution)/shard_map/all_gather | solution.py:17
  21.9 19.3 %copy-start.12 = (s32[4]{0:T(128)S(1)}, s32[4]{0:T(128)}, u32[]{:S(2)}) copy-start(s32[4]{0:T(128)} %constant.387.clone.1) | copy-start | bytes 52
  22.0 20.1 %copy-start.3 = (bf16[512,512]{1,0:T(8,128)(2,1)S(1)}, bf16[512,512]{1,0:T(8,128)(2,1)}, u32[]{:S(2)}) copy-start(bf16[512,512]{1,0:T(8,128)(2,1)} %copy-done.2) | copy-start | bytes 1572868
  30.8 185.6 %collective-permute-start.1 = (bf16[2,512,2,512]{3,1,2,0:T(8,128)(2,1)}, bf16[2,512,2,512]{3,1,2,0:T(8,128)(2,1)}, u32[]{:S(2)}, u32[]{:S(2)}) collective-permute-start(bf16[2,512,2,512]{3,1,2,0:T(8,128)(2,1)} %copy_select_fusion.2), channel_id=1, source_target_pairs={{112,0},{0,16},{16,32},{32,48},{48,64},{64,80},{80,96},{96,112},{1... | collective-permute-start | bytes 6291464 | tf_op jit(solution)/shard_map/ppermute | solution.py:13
  34.4 25.9 %collective-permute-start = (bf16[2,512,512]{2,1,0:T(8,128)(2,1)}, bf16[2,512,512]{2,1,0:T(8,128)(2,1)S(1)}, u32[]{:S(2)}, u32[]{:S(2)}) collective-permute-start(bf16[2,512,512]{2,1,0:T(8,128)(2,1)} %param.25), channel_id=1, source_target_pairs={{1,0},{2,1},{3,2},{4,3},{5,4},{6,5},{7,6},{8,7},{9,8},{10,9},{11,1... | collective-permute-start | bytes 3145736 | tf_op jit(solution)/shard_map/ppermute | solution.py:13
  225.3 2.5 copy-start.14
  225.3 2.5 copy-start.18
  228.5 0.8 copy-start.4
  229.4 104.1 %all-gather.33.cloned.1.call-start = ((), (), s32[]{:S(2)}) async-start(), calls=%async_computation.4 | async-start | bytes 8912896 | tf_op jit(solution)/shard_map/all_gather | solution.py:7
  231.5 174.5 %all-gather.35.cloned.1.call-start = ((), (), s32[]{:S(2)}) async-start(), calls=%async_computation.5 | async-start | bytes 8912896 | tf_op jit(solution)/shard_map/all_gather | solution.py:7
  232.1 229.7 %all-gather.37.cloned.1.call-start = ((), (), s32[]{:S(2)}) async-start(), calls=%async_computation.6 | async-start | bytes 4718592 | tf_op jit(solution)/shard_map/all_gather | solution.py:17
  235.2 12.3 %copy-start.5 = (bf16[512,512]{1,0:T(8,128)(2,1)S(1)}, bf16[512,512]{1,0:T(8,128)(2,1)}, u32[]{:S(2)}) copy-start(bf16[512,512]{1,0:T(8,128)(2,1)} %copy-done.4) | copy-start | bytes 1572868
  415.2 2.0 copy-start
  418.6 0.8 copy-start.6
  419.4 116.5 %all-gather.39.cloned.1.call-start = ((), (), s32[]{:S(2)}) async-start(), calls=%async_computation.7 | async-start | bytes 8912896 | tf_op jit(solution)/shard_map/all_gather | solution.py:7
  421.6 187.0 %all-gather.41.cloned.1.call-start = ((), (), s32[]{:S(2)}) async-start(), calls=%async_computation.8 | async-start | bytes 8912896 | tf_op jit(solution)/shard_map/all_gather | solution.py:7
  422.3 249.8 %all-gather.43.cloned.1.call-start = ((), (), s32[]{:S(2)}) async-start(), calls=%async_computation.9 | async-start | bytes 4718592 | tf_op jit(solution)/shard_map/all_gather | solution.py:17
  422.5 19.7 %copy-start.7 = (bf16[512,512]{1,0:T(8,128)(2,1)S(1)}, bf16[512,512]{1,0:T(8,128)(2,1)}, u32[]{:S(2)}) copy-start(bf16[512,512]{1,0:T(8,128)(2,1)} %copy-done.6) | copy-start | bytes 1572868
  431.3 182.1 %collective-permute-start.3 = (bf16[2,512,2,512]{3,1,2,0:T(8,128)(2,1)}, bf16[2,512,2,512]{3,1,2,0:T(8,128)(2,1)}, u32[]{:S(2)}, u32[]{:S(2)}) collective-permute-start(bf16[2,512,2,512]{3,1,2,0:T(8,128)(2,1)} %copy_select_fusion.1), channel_id=1, source_target_pairs={{16,0},{32,16},{48,32},{64,48},{80,64},{96,80},{112,96},{0,112},{1... | collective-permute-start | bytes 6291464 | tf_op jit(solution)/shard_map/ppermute | solution.py:13
  437.4 23.0 %collective-permute-start.2 = (bf16[2,512,512]{2,1,0:T(8,128)(2,1)}, bf16[2,512,512]{2,1,0:T(8,128)(2,1)S(1)}, u32[]{:S(2)}, u32[]{:S(2)}) collective-permute-start(bf16[2,512,512]{2,1,0:T(8,128)(2,1)} %param.25), channel_id=1, source_target_pairs={{15,0},{0,1},{1,2},{2,3},{3,4},{4,5},{5,6},{6,7},{7,8},{8,9},{9,10... | collective-permute-start | bytes 3145736 | tf_op jit(solution)/shard_map/ppermute | solution.py:13
  617.6 2.0 copy-start.1
  620.8 0.8 copy-start.8
  621.6 124.6 %all-gather.45.cloned.1.call-start = ((), (), s32[]{:S(2)}) async-start(), calls=%async_computation.10 | async-start | bytes 8912896 | tf_op jit(solution)/shard_map/all_gather | solution.py:7
  623.8 194.9 %all-gather.47.cloned.1.call-start = ((), (), s32[]{:S(2)}) async-start(), calls=%async_computation.11 | async-start | bytes 8912896 | tf_op jit(solution)/shard_map/all_gather | solution.py:7
  624.4 14.8 %copy-start.9 = (bf16[512,512]{1,0:T(8,128)(2,1)S(1)}, bf16[512,512]{1,0:T(8,128)(2,1)}, u32[]{:S(2)}) copy-start(bf16[512,512]{1,0:T(8,128)(2,1)} %copy-done.8) | copy-start | bytes 1572868
  633.2 190.4 %collective-permute-start.5 = (bf16[2,512,2,512]{3,1,2,0:T(8,128)(2,1)}, bf16[2,512,2,512]{3,1,2,0:T(8,128)(2,1)}, u32[]{:S(2)}, u32[]{:S(2)}) collective-permute-start(bf16[2,512,2,512]{3,1,2,0:T(8,128)(2,1)} %copy_select_fusion), channel_id=1, source_target_pairs={{32,0},{48,16},{64,32},{80,48},{96,64},{112,80},{0,96},{16,112},{3... | collective-permute-start | bytes 6291464 | tf_op jit(solution)/shard_map/ppermute | solution.py:13
  639.1 25.2 %collective-permute-start.4 = (bf16[2,512,512]{2,1,0:T(8,128)(2,1)}, bf16[2,512,512]{2,1,0:T(8,128)(2,1)S(1)}, u32[]{:S(2)}, u32[]{:S(2)}) collective-permute-start(bf16[2,512,512]{2,1,0:T(8,128)(2,1)} %param.25), channel_id=1, source_target_pairs={{14,0},{15,1},{0,2},{1,3},{2,4},{3,5},{4,6},{5,7},{6,8},{7,9},{8,1... | collective-permute-start | bytes 3145736 | tf_op jit(solution)/shard_map/ppermute | solution.py:13
Sparse Core Ops, SparseCore 0:
  19.0 47.5 all-gather.24
  68.8 70.0 all-gather.26
  141.0 70.4 all-gather.28
  229.5 31.0 all-gather.30
  262.6 70.8 all-gather.32
  335.5 70.4 all-gather.34
  419.5 42.2 all-gather.36
  463.9 71.8 all-gather.38
  538.0 70.4 all-gather.40
  621.7 50.3 all-gather.42
  674.3 71.8 all-gather.44
  748.2 70.4 all-gather.46
